TPU v7x, 32 devices: a whole 2x2x4 slice. The times are simulated.
32 devices in a mesh: dom: 16 (over z, y, x), st: 2 (over core).
Axes of the slice: x: 2, y: 2, z: 4, core: 2. Of those that a mesh axis runs over, the one named last changes fastest.
Arguments:
- psi: float32 [2, 16, 8, 2, 64, 256], P(None, 'dom', None, None, None, 'st'), parts along dimension 5, may hold values from -18 to 18
- potential: float32 [16, 8, 2, 64], P('dom'), may hold values from 0 to 4
Outputs:
- propagated: float32 [2, 16, 8, 2, 64, 256], P(None, 'dom', None, None, None, 'st'), parts along dimension 5
There are 2 independent parts, one for each index of `st`. A program takes and returns all parts, laid end to end along the dimension named above; an argument that names none is the same for every part. Nothing has to cross between parts.
All inputs are finite; a program needn't handle non-finite values.
Results may differ from a plain program's by a relative error of at most 0.0003.
Values sent between devices are 32-bit elements; how exact they have to be, the bound alone decides.
A program may use at most 128 MiB of HBM per device.

v0:
```python
import jax
import jax.numpy as jnp
from jax import lax
from jax.sharding import PartitionSpec as P

ITERS = 6


epsilon = 1e-06
time_step = 0.5
taylor_terms = 32
far_weight = -1.0 / 12.0
near_weight = 4.0 / 3.0
centre_weight = -7.5


def to_grid(blocked):
    parts, nblocks, cx, by, nz, orbs = blocked.shape
    grid = blocked.transpose(0, 2, 1, 3, 4, 5)
    return grid.reshape(parts, cx, nblocks * by, nz, orbs)


def to_blocks(grid, by):
    parts, nx, ny, nz, orbs = grid.shape
    blocked = grid.reshape(parts, nx, ny // by, by, nz, orbs).transpose(0, 2, 1, 3, 4, 5)
    return blocked


def shift_walls(values, offset):
    width_y = values.shape[2]
    padded = jnp.pad(values, ((0, 0), (0, 0), (2, 2), (0, 0), (0, 0)))
    return padded[:, :, 2 - offset : 2 - offset + width_y]


def hamiltonian_whole(values_in, potential):
    total = centre_weight * values_in
    for along in (1, 3):
        total = total + near_weight * (
            jnp.roll(values_in, 1, along) + jnp.roll(values_in, -1, along)
        )
        total = total + far_weight * (
            jnp.roll(values_in, 2, along) + jnp.roll(values_in, -2, along)
        )
    total = total + near_weight * (shift_walls(values_in, 1) + shift_walls(values_in, -1))
    total = total + far_weight * (shift_walls(values_in, 2) + shift_walls(values_in, -2))
    return -0.5 * total + potential[None, :, :, :, None] * values_in


def tridiagonal(alphas, betas, vector):
    zero_row = jnp.zeros((1, vector.shape[1]), jnp.float32)
    upper = jnp.concatenate([betas * vector[1:], zero_row], axis=0)
    lower = jnp.concatenate([zero_row, betas * vector[:-1]], axis=0)
    return alphas * vector + upper + lower


def krylov_exponential(alphas, betas):
    count = alphas.shape[0]
    first = (jnp.arange(count) == 0).astype(jnp.float32)[:, None] * jnp.ones_like(alphas)
    term_real = first
    term_imag = jnp.zeros_like(alphas)
    sum_real = term_real
    sum_imag = term_imag
    for order in range(1, taylor_terms):
        applied_real = tridiagonal(alphas, betas, term_real)
        applied_imag = tridiagonal(alphas, betas, term_imag)
        term_real = time_step * applied_imag / order
        term_imag = -time_step * applied_real / order
        sum_real = sum_real + term_real
        sum_imag = sum_imag + term_imag
    return (sum_real, sum_imag)


def combine_basis(krylov_basis, alpha_list, beta_list, first_norm):
    coef_real, coef_imag = krylov_exponential(jnp.stack(alpha_list), jnp.stack(beta_list))
    out_real = jnp.zeros_like(krylov_basis[0][0])
    out_imag = jnp.zeros_like(krylov_basis[0][0])
    for index_j in range(len(krylov_basis)):
        basis_now = krylov_basis[index_j]
        out_real = out_real + coef_real[index_j] * basis_now[0] - coef_imag[index_j] * basis_now[1]
        out_imag = out_imag + coef_real[index_j] * basis_now[1] + coef_imag[index_j] * basis_now[0]
    return first_norm * jnp.stack([out_real, out_imag])


def local_lanczos(grid_psi, grid_pot):
    axes_all = (0, 1, 2, 3)
    first_norm = jnp.sqrt(jnp.sum(grid_psi * grid_psi, axis=axes_all) + epsilon)
    vector = grid_psi / first_norm
    previous = jnp.zeros_like(vector)
    beta_prev = jnp.zeros_like(first_norm)
    krylov_basis = []
    alpha_list = []
    beta_list = []
    for iteration in range(ITERS):
        applied = hamiltonian_whole(vector, grid_pot)
        alpha_now = jnp.sum(vector * applied, axis=axes_all)
        krylov_basis.append(vector)
        alpha_list.append(alpha_now)
        if iteration + 1 < ITERS:
            remainder = applied - alpha_now * vector - beta_prev * previous
            beta_now = jnp.sqrt(jnp.sum(remainder * remainder, axis=axes_all) + epsilon)
            previous = vector
            vector = remainder / beta_now
            beta_prev = beta_now
            beta_list.append(beta_now)
    return combine_basis(krylov_basis, alpha_list, beta_list, first_norm)


def on_device(psi, potential):
    by = psi.shape[3]
    moved = lax.all_to_all(psi, "dom", split_axis=5, concat_axis=1, tiled=True)
    whole_pot = lax.all_gather(potential, "dom", axis=0, tiled=True)
    grid_pot = to_grid(whole_pot[None, :, :, :, :, None])[0, :, :, :, 0]
    result = to_blocks(local_lanczos(to_grid(moved), grid_pot), by)
    return lax.all_to_all(result, "dom", split_axis=1, concat_axis=5, tiled=True)


def solution(mesh):
    placed = (P(None, "dom", None, None, None, "st"), P("dom", None, None, None))
    return jax.shard_map(
        on_device,
        mesh=mesh,
        in_specs=placed,
        out_specs=P(None, "dom", None, None, None, "st"),
        check_vma=False,
    )
```

profile of v0, /device:TPU:0, one launch (start us, length us, event | category | flops | bytes accessed | tf_op | source)
XLA Modules:
  0.0 273.2 jit_solution(6552418188580268950)
XLA Ops:
  0.0 3.3 %copy.9 = f32[2,1,8,2,64,128]{4,3,2,0,1,5:T(2,128)S(1)} copy(f32[2,1,8,2,64,128]{5,4,3,2,1,0:T(8,128)} %param.2) | data formatting | bytes 2097152 | tf_op args[0]
  3.3 3.2 %reshape.127 = f32[16,1,16384]{2,1,0:T(1,128)} reshape(f32[128,1,2,8,2,64]{5,4,3,2,1,0:T(2,128)S(1)} %bitcast.86) | data formatting | bytes 2097152
  6.5 8.3 %all-to-all-start = ((f32[16,1,16384]{2,1,0:T(1,128)}), f32[16,1,16384]{2,1,0:T(1,128)S(1)}, u32[]{:S(2)}, u32[]{:S(2)}) async-start(f32[16,1,16384]{2,1,0:T(1,128)} %reshape.127), calls=%async_computation | async-start | bytes 2097152 | tf_op jit(solution)/shard_map/all_to_all | solution.py:110
  14.9 51.6 %all_gather.3 = f32[16,8,2,64]{3,1,2,0:T(8,128)S(1)} all-gather(f32[1,8,2,64]{3,1,2,0:T(8,128)S(1)} %copy.12), channel_id=1, replica_groups=mesh['dom'=16,'st'=2] {'dom'}, dimensions={0}, use_global_device_ids=true | all-gather | bytes 69632 | tf_op jit(solution)/shard_map/all_gather | solution.py:111
  68.3 3.2 %reduce.1 = f32[16,16384]{1,0:T(8,128)S(1)} reduce(f32[16,1,16384]{2,1,0:T(1,128)S(1)} %all-to-all-done, f32[]{:T(128)} %broadcast.625), dimensions={1}, to_apply=%all_to_all.26.reduce_sub_computation | reduce | bytes 2097156 | tf_op jit(solution)/shard_map/all_to_all | solution.py:110
  79.0 2.7 fusion.155
  81.6 2.7 %fusion.156 = (f32[2,8,32,62,8]{3,4,2,1,0:T(8,128)}, f32[2,8,32,62,8]{3,4,2,1,0:T(8,128)}) fusion(f32[2,8,32,64,8]{3,4,2,1,0:T(8,128)S(1)} %broadcast_divide_fusion.5), kind=kLoop, calls=%fused_computation.433 | loop fusion | bytes 4063232 | tf_op jit(solution)/shard_map/jit(_roll_static)/slice | solution.py:42
  90.0 8.1 %multiply_reduce_fusion.9 = (f32[8]{0:T(128)S(1)}, f32[2,8,32,64,8]{3,4,2,1,0:T(8,128)S(1)}) fusion(f32[2,8,32,64,8]{3,4,2,1,0:T(8,128)S(1)} %broadcast_divide_fusion.5, f32[8,32,64]{2,1,0:T(8,128)S(1)} %copy.13, f32[2,8,32,2,8]{3,4,2,1,0:T(8,128)} %get-tuple-element.118, f32[2,8,32,62,8]{3,4,2,1,0:T(8,128)} %get-tuple-element.120, ...), kind=kLoop, calls=%fused_computation.163 | loop fusion | flops 8388600 | bytes 10551328 | tf_op jit(solution)/shard_map/reduce_sum | solution.py:95
  102.1 2.7 fusion.148
  104.8 2.8 %fusion.145 = (f32[2,8,32,1,8]{3,4,2,1,0:T(8,128)}, f32[2,8,32,1,8]{3,4,2,1,0:T(8,128)}) fusion(f32[2,8,32,64,8]{3,4,2,1,0:T(8,128)S(1)} %broadcast_divide_fusion.4), kind=kLoop, calls=%fused_computation.422 | loop fusion | bytes 65536 | tf_op jit(solution)/shard_map/jit(_roll_static)/slice | solution.py:39
  113.2 8.2 %multiply_reduce_fusion.7 = (f32[8]{0:T(128)S(1)}, f32[2,8,32,64,8]{3,4,2,1,0:T(8,128)S(1)}) fusion(f32[2,8,32,64,8]{3,4,2,1,0:T(8,128)S(1)} %broadcast_divide_fusion.4, f32[8,32,64]{2,1,0:T(8,128)S(1)} %copy.13, f32[2,8,32,2,8]{3,4,2,1,0:T(8,128)} %get-tuple-element.102, f32[2,8,32,62,8]{3,4,2,1,0:T(8,128)} %get-tuple-element.104, ...), kind=kLoop, calls=%fused_computation.160 | loop fusion | flops 8388600 | bytes 10551328 | tf_op jit(solution)/shard_map/reduce_sum | solution.py:95
  123.4 2.7 fusion.138
  126.1 2.8 %fusion.139 = (f32[2,8,32,2,8]{3,4,2,1,0:T(8,128)}, f32[2,8,32,2,8]{3,4,2,1,0:T(8,128)}) fusion(f32[2,8,32,64,8]{3,4,2,1,0:T(8,128)S(1)} %broadcast_divide_fusion.3), kind=kLoop, calls=%fused_computation.416 | loop fusion | bytes 131072 | tf_op jit(solution)/shard_map/jit(_roll_static)/slice | solution.py:42
  128.9 2.8 %fusion.140 = (f32[2,8,32,62,8]{3,4,2,1,0:T(8,128)}, f32[2,8,32,62,8]{3,4,2,1,0:T(8,128)}) fusion(f32[2,8,32,64,8]{3,4,2,1,0:T(8,128)S(1)} %broadcast_divide_fusion.3), kind=kLoop, calls=%fused_computation.417 | loop fusion | bytes 4063232 | tf_op jit(solution)/shard_map/jit(_roll_static)/slice | solution.py:42
  137.4 8.5 %multiply_reduce_fusion.5 = (f32[8]{0:T(128)S(1)}, f32[2,8,32,64,8]{3,4,2,1,0:T(8,128)S(1)}) fusion(f32[2,8,32,64,8]{3,4,2,1,0:T(8,128)S(1)} %broadcast_divide_fusion.3, f32[8,32,64]{2,1,0:T(8,128)S(1)} %copy.13, f32[2,8,32,2,8]{3,4,2,1,0:T(8,128)} %get-tuple-element.86, f32[2,8,32,62,8]{3,4,2,1,0:T(8,128)} %get-tuple-element.88, ...), kind=kLoop, calls=%fused_computation.157 | loop fusion | flops 8388600 | bytes 10551328 | tf_op jit(solution)/shard_map/reduce_sum | solution.py:95
  149.3 2.8 %fusion.130 = (f32[2,8,32,63,8]{3,4,2,1,0:T(8,128)}, f32[2,8,32,63,8]{3,4,2,1,0:T(8,128)}) fusion(f32[2,8,32,64,8]{3,4,2,1,0:T(8,128)S(1)} %broadcast_divide_fusion.2), kind=kLoop, calls=%fused_computation.407 | loop fusion | bytes 4128768 | tf_op jit(solution)/shard_map/jit(_roll_static)/slice | solution.py:39
  152.1 2.8 %fusion.131 = (f32[2,8,32,2,8]{3,4,2,1,0:T(8,128)}, f32[2,8,32,2,8]{3,4,2,1,0:T(8,128)}) fusion(f32[2,8,32,64,8]{3,4,2,1,0:T(8,128)S(1)} %broadcast_divide_fusion.2), kind=kLoop, calls=%fused_computation.408 | loop fusion | bytes 131072 | tf_op jit(solution)/shard_map/jit(_roll_static)/slice | solution.py:42
  154.9 2.8 %fusion.132 = (f32[2,8,32,62,8]{3,4,2,1,0:T(8,128)}, f32[2,8,32,62,8]{3,4,2,1,0:T(8,128)}) fusion(f32[2,8,32,64,8]{3,4,2,1,0:T(8,128)S(1)} %broadcast_divide_fusion.2), kind=kLoop, calls=%fused_computation.409 | loop fusion | bytes 4063232 | tf_op jit(solution)/shard_map/jit(_roll_static)/slice | solution.py:42
  163.4 9.2 %multiply_reduce_fusion.3 = (f32[8]{0:T(128)S(1)}, f32[2,8,32,64,8]{3,4,2,1,0:T(8,128)S(1)}) fusion(f32[2,8,32,64,8]{3,4,2,1,0:T(8,128)S(1)} %broadcast_divide_fusion.2, f32[8,32,64]{2,1,0:T(8,128)S(1)} %copy.13, f32[2,8,32,2,8]{3,4,2,1,0:T(8,128)} %get-tuple-element.70, f32[2,8,32,62,8]{3,4,2,1,0:T(8,128)} %get-tuple-element.72, ...), kind=kLoop, calls=%fused_computation.154 | loop fusion | flops 8388600 | bytes 10551328 | tf_op jit(solution)/shard_map/reduce_sum | solution.py:95
  176.2 2.7 fusion.122
  178.9 2.8 %fusion.123 = (f32[2,8,32,2,8]{3,4,2,1,0:T(8,128)}, f32[2,8,32,2,8]{3,4,2,1,0:T(8,128)}) fusion(f32[2,8,32,64,8]{3,4,2,1,0:T(8,128)S(1)} %broadcast_divide_fusion.1), kind=kLoop, calls=%fused_computation.400 | loop fusion | bytes 131072 | tf_op jit(solution)/shard_map/jit(_roll_static)/slice | solution.py:42
  181.7 2.7 fusion.124
  190.3 9.3 %multiply_reduce_fusion.1 = (f32[8]{0:T(128)S(1)}, f32[2,8,32,64,8]{3,4,2,1,0:T(8,128)S(1)}) fusion(f32[2,8,32,64,8]{3,4,2,1,0:T(8,128)S(1)} %broadcast_divide_fusion.1, f32[8,32,64]{2,1,0:T(8,128)S(1)} %copy.13, f32[2,8,32,2,8]{3,4,2,1,0:T(8,128)} %get-tuple-element.54, f32[2,8,32,62,8]{3,4,2,1,0:T(8,128)} %get-tuple-element.56, ...), kind=kLoop, calls=%fused_computation.151 | loop fusion | flops 8388600 | bytes 10551328 | tf_op jit(solution)/shard_map/reduce_sum | solution.py:95
  200.9 2.7 fusion.113
  203.7 2.8 %fusion.114 = (f32[2,8,32,63,8]{3,4,2,1,0:T(8,128)}, f32[2,8,32,63,8]{3,4,2,1,0:T(8,128)}) fusion(f32[2,8,32,64,8]{3,4,2,1,0:T(8,128)S(1)} %broadcast_divide_fusion), kind=kLoop, calls=%fused_computation.391 | loop fusion | bytes 4128768 | tf_op jit(solution)/shard_map/jit(_roll_static)/slice | solution.py:39
  206.5 2.7 fusion.115
  209.2 2.7 fusion.116
  217.3 13.3 %fusion.98 = f32[8]{0:T(128)S(1)} fusion(f32[2,8,32,64,8]{3,4,2,1,0:T(8,128)} %copy-done, f32[2,8,32,2,8]{3,4,2,1,0:T(8,128)} %get-tuple-element.38, f32[2,8,32,62,8]{3,4,2,1,0:T(8,128)} %get-tuple-element.40, f32[2,8,32,62,8]{3,4,2,1,0:T(8,128)} %get-tuple-element.39, f32[2,8,32,2,8]{3,4,2,1,0:T(8,128)} %get-tuple-element.37, ...), kind=kLoop, calls=%fused_computation.165 | loop fusion | flops 8388600 | bytes 9502752 | tf_op jit(solution)/shard_map/reduce_sum | solution.py:95
  232.3 4.9 %multiply_subtract_fusion.5 = f32[1,8,32,64,8]{3,4,2,1,0:T(8,128)S(1)} fusion(f32[2,8,32,64,8]{3,4,2,1,0:T(8,128)S(1)} %copy-done.1, f32[2,8,32,64,8]{3,4,2,1,0:T(8,128)} %copy-done.8, f32[2,8,32,64,8]{3,4,2,1,0:T(8,128)} %copy-done.6, f32[2,8,32,64,8]{3,4,2,1,0:T(8,128)} %copy-done.4, f32[2,8,32,64,8]{3,4,2,1,0:T(8,128)S(1)} %broadcast_divide_fusion.4, ...), kind=kLoop, calls=%fused_computation.167 | loop fusion | flops 3014656 | bytes 6816128 | tf_op jit(solution)/shard_map/sub | solution.py:79
  241.2 22.9 %all_to_all.36 = f32[16,1,16384]{2,1,0:T(1,128)S(1)} all-to-all(f32[16,1,16384]{2,1,0:T(1,128)S(1)} %reshape.129), channel_id=1, replica_groups=mesh['dom'=16,'st'=2] {'dom'}, dimensions={0} | all-to-all | bytes 2097152 | tf_op jit(solution)/shard_map/all_to_all | solution.py:114
  264.2 3.2 %reduce.2 = f32[16,16384]{1,0:T(8,128)S(1)} reduce(f32[16,1,16384]{2,1,0:T(1,128)S(1)} %all_to_all.36, f32[]{:T(128)} %broadcast.625), dimensions={1}, to_apply=%all_to_all.30.reduce_sub_computation | reduce | bytes 2097156 | tf_op jit(solution)/shard_map/all_to_all | solution.py:114
  269.8 3.1 %copy.16 = f32[2,1,8,2,64,128]{5,4,3,2,1,0:T(8,128)} copy(f32[2,1,8,2,64,128]{4,5,3,2,0,1:T(8,128)} %copy_bitcast_fusion) | data formatting | bytes 2097152 | tf_op jit(solution)/shard_map/all_to_all | solution.py:114
  (159 shorter events, 65.0 us)
Async XLA Ops:
  3.3 11.5 %copy-start.10 = (f32[1,8,2,64]{3,2,1,0:T(2,128)S(1)}, f32[1,8,2,64]{3,2,1,0:T(2,128)}, u32[]{:S(2)}) copy-start(f32[1,8,2,64]{3,2,1,0:T(2,128)} %param.3) | copy-start | bytes 12292
  6.5 61.2 %all-to-all-start = ((f32[16,1,16384]{2,1,0:T(1,128)}), f32[16,1,16384]{2,1,0:T(1,128)S(1)}, u32[]{:S(2)}, u32[]{:S(2)}) async-start(f32[16,1,16384]{2,1,0:T(1,128)} %reshape.127), calls=%async_computation | async-start | bytes 2097152 | tf_op jit(solution)/shard_map/all_to_all | solution.py:110
  76.0 14.0 %copy-start.2 = (f32[2,8,32,64,8]{3,4,2,1,0:T(8,128)}, f32[2,8,32,64,8]{3,4,2,1,0:T(8,128)S(1)}, u32[]{:S(2)}) copy-start(f32[2,8,32,64,8]{3,4,2,1,0:T(8,128)S(1)} %broadcast_divide_fusion.5) | copy-start | bytes 3145732
  122.7 14.7 %copy-start.4 = (f32[2,8,32,64,8]{3,4,2,1,0:T(8,128)}, f32[2,8,32,64,8]{3,4,2,1,0:T(8,128)S(1)}, u32[]{:S(2)}) copy-start(f32[2,8,32,64,8]{3,4,2,1,0:T(8,128)S(1)} %broadcast_divide_fusion.3) | copy-start | bytes 3145732
  147.2 16.2 %copy-start.6 = (f32[2,8,32,64,8]{3,4,2,1,0:T(8,128)}, f32[2,8,32,64,8]{3,4,2,1,0:T(8,128)S(1)}, u32[]{:S(2)}) copy-start(f32[2,8,32,64,8]{3,4,2,1,0:T(8,128)S(1)} %broadcast_divide_fusion.2) | copy-start | bytes 3145732
  174.1 16.2 %copy-start.8 = (f32[2,8,32,64,8]{3,4,2,1,0:T(8,128)}, f32[2,8,32,64,8]{3,4,2,1,0:T(8,128)S(1)}, u32[]{:S(2)}) copy-start(f32[2,8,32,64,8]{3,4,2,1,0:T(8,128)S(1)} %broadcast_divide_fusion.1) | copy-start | bytes 3145732
  200.9 15.5 %copy-start = (f32[2,8,32,64,8]{3,4,2,1,0:T(8,128)}, f32[2,8,32,64,8]{3,4,2,1,0:T(8,128)S(1)}, u32[]{:S(2)}) copy-start(f32[2,8,32,64,8]{3,4,2,1,0:T(8,128)S(1)} %broadcast_divide_fusion) | copy-start | bytes 3145732
  217.3 13.4 %copy-start.12 = (f32[5]{0:T(128)S(1)}, f32[5]{0:T(128)}, u32[]{:S(2)}) copy-start(f32[5]{0:T(128)} %get-tuple-element.371) | copy-start | bytes 64
  217.3 13.4 %copy-start.13 = (f32[5]{0:T(128)S(1)}, f32[5]{0:T(128)}, u32[]{:S(2)}) copy-start(f32[5]{0:T(128)} %get-tuple-element.372) | copy-start | bytes 64
  217.3 13.5 %copy-start.11 = (f32[6]{0:T(128)S(1)}, f32[6]{0:T(128)}, u32[]{:S(2)}) copy-start(f32[6]{0:T(128)} %compare_convert_fusion.1) | copy-start | bytes 76
  230.7 1.6 copy-start.1
  232.3 4.9 %copy-start.3 = (f32[2,8,32,64,8]{3,4,2,1,0:T(8,128)S(1)}, f32[2,8,32,64,8]{3,4,2,1,0:T(8,128)}, u32[]{:S(2)}) copy-start(f32[2,8,32,64,8]{3,4,2,1,0:T(8,128)} %copy-done.2) | copy-start | bytes 3145732
  232.3 4.9 %copy-start.5 = (f32[2,8,32,64,8]{3,4,2,1,0:T(8,128)S(1)}, f32[2,8,32,64,8]{3,4,2,1,0:T(8,128)}, u32[]{:S(2)}) copy-start(f32[2,8,32,64,8]{3,4,2,1,0:T(8,128)} %copy-done.4) | copy-start | bytes 3145732
  232.3 5.3 %copy-start.7 = (f32[2,8,32,64,8]{3,4,2,1,0:T(8,128)S(1)}, f32[2,8,32,64,8]{3,4,2,1,0:T(8,128)}, u32[]{:S(2)}) copy-start(f32[2,8,32,64,8]{3,4,2,1,0:T(8,128)} %copy-done.6) | copy-start | bytes 3145732
  232.3 5.9 %copy-start.9 = (f32[2,8,32,64,8]{3,4,2,1,0:T(8,128)S(1)}, f32[2,8,32,64,8]{3,4,2,1,0:T(8,128)}, u32[]{:S(2)}) copy-start(f32[2,8,32,64,8]{3,4,2,1,0:T(8,128)} %copy-done.8) | copy-start | bytes 3145732
where the time goes:
time: 276 us; the launch traced here: 273 us
  local copies, waits for them, and re-layouts  110 us (40%)
  other arithmetic  79.3 us (29%)
  blocking collectives  74.6 us (27%)
  starting transfers between devices  8.34 us (3%)
    reduce_sum x6, other arithmetic, local_lanczos(): alpha_now = jnp.sum(vector * applied, axis=axes_all)  56.6 us
    all_gather x1, blocking collectives, on_device(): whole_pot = lax.all_gather(potential, 'dom', axis=0, tiled=True)  51.6 us
    slice x24, local copies, waits for them, and re-layouts, hamiltonian_whole(): jnp.roll(values_in, 2, along) + jnp.roll(values_in, -2, along)  50.2 us
    slice x24, local copies, waits for them, and re-layouts, hamiltonian_whole(): jnp.roll(values_in, 1, along) + jnp.roll(values_in, -1, along)  41 us
    all_to_all x1, blocking collectives, on_device(): lax.all_to_all(result, 'dom', split_axis=1, concat_axis=5, tiled=True)  22.9 us
    unnamed x34, local copies, waits for them, and re-layouts  11.3 us
    all_to_all x1, starting transfers between devices, on_device(): moved = lax.all_to_all(psi, 'dom', split_axis=5, concat_axis=1, tiled=True)  8.34 us
  transfers between devices with their start and end apart: 1, of which 0 were waited for; matrix products, arithmetic and copies ran while one was open for 0% of the time, Pallas kernels for 0%

commit v1 on v0

--- a/solution.py
+++ b/solution.py
@@ -1,6 +1,10 @@
+import functools
+
 import jax
 import jax.numpy as jnp
 from jax import lax
+from jax.experimental import pallas as pl
+from jax.experimental.pallas import tpu as pltpu
 from jax.sharding import PartitionSpec as P
 
 ITERS = 6
@@ -114,10 +118,308 @@
     return lax.all_to_all(result, "dom", split_axis=1, concat_axis=5, tiled=True)
 
 
+SUB = 8
+LANES = 128
+HALF = SUB // 2
+CHUNKS = 2
+UNROLL_A = 2
+UNROLL_B = 2
+
+
+def swap_parts(x):
+    return pltpu.roll(x, HALF, 0)
+
+
+def total_of(acc):
+    summed = jnp.broadcast_to(jnp.sum(acc, axis=1, keepdims=True), (SUB, LANES))
+    return summed + swap_parts(summed)
+
+
+def krylov_weights(alphas, betas):
+    count = len(alphas)
+    one = jnp.ones((SUB, LANES), jnp.float32)
+    term = [one] + [None] * (count - 1)
+    real = [one] + [None] * (count - 1)
+    imag = [None] * count
+    for order in range(1, taylor_terms):
+        fresh = []
+        for i in range(count):
+            pieces = []
+            if term[i] is not None:
+                pieces.append(alphas[i] * term[i])
+            if i + 1 < count and term[i + 1] is not None:
+                pieces.append(betas[i] * term[i + 1])
+            if i > 0 and term[i - 1] is not None:
+                pieces.append(betas[i - 1] * term[i - 1])
+            fresh.append(sum(pieces[1:], pieces[0]) * (time_step / order) if pieces else None)
+        term = fresh
+        into = imag if order % 2 else real
+        minus = order % 4 in (1, 2)
+        for i in range(count):
+            if term[i] is not None:
+                if into[i] is None:
+                    into[i] = -term[i] if minus else term[i]
+                else:
+                    into[i] = into[i] - term[i] if minus else into[i] + term[i]
+    zero = jnp.zeros((SUB, LANES), jnp.float32)
+    return [zero if r is None else r for r in real], [zero if m is None else m for m in imag]
+
+
+def kernel(n, nx, nz, psi_ref, pot_ref, out_ref, send, recv, basis, outb, back, pots,
+           send_sem, recv_sem, pot_send, pot_recv, back_send, back_recv):
+    me = lax.axis_index("dom")
+    mesh_ids = pl.DeviceIdType.MESH
+    barrier = pltpu.get_barrier_semaphore()
+
+    def greet(k, carry):
+        pl.semaphore_signal(barrier, inc=1, device_id={"dom": lax.rem(me + k, n)}, device_id_type=mesh_ids)
+        return carry
+
+    lax.fori_loop(1, n, greet, 0)
+
+    def forward(c, here, there):
+        return pltpu.make_async_remote_copy(
+            src_ref=send.at[c, there], dst_ref=recv.at[c, here + 1],
+            send_sem=send_sem.at[c, there], recv_sem=recv_sem.at[c, here],
+            device_id={"dom": there}, device_id_type=mesh_ids)
+
+    def pot_copy(here, there):
+        return pltpu.make_async_remote_copy(
+            src_ref=pot_ref, dst_ref=pots.at[here],
+            send_sem=pot_send.at[there], recv_sem=pot_recv.at[here],
+            device_id={"dom": there}, device_id_type=mesh_ids)
+
+    def backward(c, here, there):
+        return pltpu.make_async_remote_copy(
+            src_ref=outb.at[c, there], dst_ref=back.at[c, here],
+            send_sem=back_send.at[c, there], recv_sem=back_recv.at[c, here],
+            device_id={"dom": there}, device_id_type=mesh_ids)
+
+    low = lax.broadcasted_iota(jnp.int32, (n, SUB, LANES), 1) < HALF
+
+    def interleave(a, b):
+        return (jnp.where(low, a, pltpu.roll(b, HALF, 1)), jnp.where(low, pltpu.roll(a, HALF, 1), b))
+
+    def pack(x, carry):
+        parts = [psi_ref[p * nx + x].T.reshape(n, SUB, LANES) for p in range(2)]
+        for c, block in enumerate(interleave(*parts)):
+            send[c, :, x] = block
+        return carry
+
+    lax.fori_loop(0, nx, pack, 0)
+
+    pots[me] = pot_ref[...]
+    blank = jnp.zeros((nx, SUB, LANES), jnp.float32)
+    for c in range(CHUNKS):
+        recv[c, me + 1] = send[c, me]
+        recv[c, 0] = blank
+        recv[c, n + 1] = blank
+    for j in range(ITERS - 1):
+        basis[j, 0] = blank
+        basis[j, n + 1] = blank
+
+    pl.semaphore_wait(barrier, n - 1)
+
+    def send_pot(k, carry):
+        pot_copy(me, lax.rem(me + k, n)).start()
+        return carry
+
+    lax.fori_loop(1, n, send_pot, 0)
+    for c in range(CHUNKS):
+        def send_one(k, carry, c=c):
+            forward(c, me, lax.rem(me + k, n)).start()
+            return carry
+
+        lax.fori_loop(1, n, send_one, 0)
+
+    def wait_pot(k, carry):
+        there = lax.rem(me + n - k, n)
+        pot_copy(there, there).wait_recv()
+        return carry
+
+    lane = lax.broadcasted_iota(jnp.int32, (SUB, LANES), 1)
+    upper = lane >= nz
+    cell = lax.rem(lane, nz)
+    sign = jnp.where(lax.broadcasted_iota(jnp.int32, (SUB, LANES), 0) < HALF, 1.0, -1.0)
+    masks = {1: cell < 1, 2: cell < 2, -1: cell >= nz - 1, -2: cell >= nz - 2}
+    near, far = -0.5 * near_weight, -0.5 * far_weight
+    rotate = lambda u, by: pltpu.roll(u, by % LANES, 1)
+
+    def along_z(u, by):
+        return jnp.where(masks[by], rotate(u, by + nz), rotate(u, by))
+
+    def applied_at(ref, s):
+        before = [ref[s, x] for x in range(nx)]
+        now = [ref[s + 1, x] for x in range(nx)]
+        after = [ref[s + 2, x] for x in range(nx)]
+        result = []
+        for x in range(nx):
+            u = now[x]
+            close = now[(x + 1) % nx] + now[(x - 1) % nx]
+            close = close + rotate(u + jnp.where(upper, before[x], after[x]), nz)
+            close = close + along_z(u, 1) + along_z(u, -1)
+            wide = now[(x + 2) % nx] + now[(x - 2) % nx] + before[x] + after[x]
+            wide = wide + along_z(u, 2) + along_z(u, -2)
+            own = jnp.broadcast_to(pots[s, pl.ds(x, 1), :], (SUB, LANES)) + -0.5 * centre_weight
+            result.append(own * u + near * close + far * wide)
+        return now, result
+
+    def chunk(c, carry):
+        vectors = [recv.at[c]] + [basis.at[j] for j in range(ITERS - 1)]
+
+        def arrive(k, acc):
+            there = lax.rem(me + n - k, n)
+            forward(c, there, there).wait_recv()
+            for x in range(nx):
+                u = recv[c, there + 1, x]
+                acc = acc + u * u
+            return acc
+
+        acc = jnp.zeros((SUB, LANES), jnp.float32)
+        for x in range(nx):
+            u = recv[c, me + 1, x]
+            acc = acc + u * u
+        acc = lax.fori_loop(1, n, arrive, acc)
+        first_norm = jnp.sqrt(total_of(acc) + epsilon)
+
+        @pl.when(c == 0)
+        def _():
+            lax.fori_loop(1, n, wait_pot, 0)
+
+        scales = [1.0 / first_norm]
+        alphas, betas = [], []
+        zero = jnp.zeros((SUB, LANES), jnp.float32)
+        for j in range(ITERS):
+            ref = vectors[j]
+            last = j + 1 == ITERS
+            fresh = None if last else vectors[j + 1]
+
+            def apply(s, accs, ref=ref, fresh=fresh):
+                accs = list(accs)
+                now, result = applied_at(ref, s)
+                for x in range(nx):
+                    if fresh is not None:
+                        fresh[s + 1, x] = result[x]
+                    accs[x % 2] = accs[x % 2] + now[x] * result[x]
+                return tuple(accs)
+
+            accs = lax.fori_loop(0, n, apply, (zero, zero), unroll=UNROLL_A)
+            scale = scales[j]
+            alpha = scale * (scale * total_of(accs[0] + accs[1]))
+            alphas.append(alpha)
+            if last:
+                break
+            by_self = alpha * scale
+            by_previous = betas[j - 1] * scales[j - 1] if j else None
+
+            def reduce(s, accs, ref=ref, fresh=fresh, scale=scale, by_self=by_self, by_previous=by_previous, j=j):
+                accs = list(accs)
+                for x in range(nx):
+                    r = scale * fresh[s + 1, x] - by_self * ref[s + 1, x]
+                    if j:
+                        r = r - by_previous * vectors[j - 1][s + 1, x]
+                    fresh[s + 1, x] = r
+                    accs[x % 2] = accs[x % 2] + r * r
+                return tuple(accs)
+
+            accs = lax.fori_loop(0, n, reduce, (zero, zero), unroll=UNROLL_B)
+            beta = jnp.sqrt(total_of(accs[0] + accs[1]) + epsilon)
+            betas.append(beta)
+            scales.append(1.0 / beta)
+
+        real, imag = krylov_weights(alphas, betas)
+        straight = [first_norm * scales[j] * real[j] for j in range(ITERS)]
+        crossed = [first_norm * scales[j] * imag[j] * sign for j in range(ITERS)]
+
+        def combined(d, x):
+            us = [v[d + 1, x] for v in vectors]
+            a = straight[0] * us[0]
+            b = crossed[0] * us[0]
+            for j in range(1, ITERS):
+                a = a + straight[j] * us[j]
+                b = b + crossed[j] * us[j]
+            return a + swap_parts(b)
+
+        def finish(k, carry):
+            there = lax.rem(me + k, n)
+            for x in range(nx):
+                outb[c, there, x] = combined(there, x)
+
+            @pl.when(k > 1)
+            def _():
+                backward(c, me, lax.rem(me + k - 1, n)).start()
+
+            return carry
+
+        lax.fori_loop(1, n, finish, 0)
+        for x in range(nx):
+            back[c, me, x] = combined(me, x)
+        backward(c, me, lax.rem(me + n - 1, n)).start()
+        return carry
+
+    lax.fori_loop(0, CHUNKS, chunk, 0)
+
+    for c in range(CHUNKS):
+        def returned(k, carry, c=c):
+            there = lax.rem(me + n - k, n)
+            backward(c, there, there).wait_recv()
+            return carry
+
+        lax.fori_loop(1, n, returned, 0)
+
+    def unpack(x, carry):
+        for p, block in enumerate(interleave(back[0, :, x], back[1, :, x])):
+            out_ref[p * nx + x] = block.reshape(n * SUB, LANES).T
+        return carry
+
+    lax.fori_loop(0, nx, unpack, 0)
+
+    def sent(k, carry):
+        there = lax.rem(me + k, n)
+        pot_copy(me, there).wait_send()
+        for c in range(CHUNKS):
+            forward(c, me, there).wait_send()
+            backward(c, me, there).wait_send()
+        return carry
+
+    lax.fori_loop(1, n, sent, 0)
+
+
+def fused(psi, potential, n):
+    parts, slabs, nx, by, nz, orbs = psi.shape
+    rows = nx * by * nz // LANES
+    vec = lambda *lead: pltpu.VMEM(lead + (nx, SUB, LANES), jnp.float32)
+    dma = lambda *shape: pltpu.SemaphoreType.DMA(shape)
+    result = pl.pallas_call(
+        functools.partial(kernel, n, nx, nz),
+        out_shape=jax.ShapeDtypeStruct((parts * nx, by * nz, orbs), jnp.float32),
+        in_specs=[pl.BlockSpec(memory_space=pltpu.VMEM)] * 2,
+        out_specs=pl.BlockSpec(memory_space=pltpu.VMEM),
+        scratch_shapes=[
+            vec(CHUNKS, n), vec(CHUNKS, n + 2), vec(ITERS - 1, n + 2), vec(CHUNKS, n), vec(CHUNKS, n),
+            pltpu.VMEM((n, nx, LANES), jnp.float32),
+            dma(CHUNKS, n), dma(CHUNKS, n), dma(n), dma(n), dma(CHUNKS, n), dma(CHUNKS, n),
+        ],
+        compiler_params=pltpu.CompilerParams(collective_id=0, has_side_effects=True),
+    )(psi.reshape(parts * nx, by * nz, orbs), potential.reshape(nx, by * nz))
+    return result.reshape(psi.shape)
+
+
+def fits(psi, n):
+    parts, slabs, nx, by, nz, orbs = psi.shape
+    return parts == 2 and slabs == 1 and by == 2 and by * nz == LANES and orbs == LANES and orbs == n * SUB and n > 1
+
+
+def per_device(n, psi, potential):
+    if fits(psi, n):
+        return fused(psi, potential, n)
+    return on_device(psi, potential)
+
+
 def solution(mesh):
     placed = (P(None, "dom", None, None, None, "st"), P("dom", None, None, None))
     return jax.shard_map(
-        on_device,
+        functools.partial(per_device, mesh.shape["dom"]),
         mesh=mesh,
         in_specs=placed,
         out_specs=P(None, "dom", None, None, None, "st"),

time: 276 us -> 70.8 us (0.26)
  the two profiles are of different devices: /device:TPU:0 before, /device:TPU:28 now
where the time goes in v1:
time: 70.8 us; the launch traced here: 70.5 us
  Pallas kernels  66.9 us (94%)
  local copies, waits for them, and re-layouts  3.67 us (5%)
    pallas_call x1, Pallas kernels, fused(): pl.pallas_call(functools.partial(kernel, n, nx, nz), out_shape=jax.ShapeD...  66.9 us
    unnamed x1, local copies, waits for them, and re-layouts  2.31 us

profile of v1, /device:TPU:28, one launch (start us, length us, event | category | flops | bytes accessed | tf_op | source)
XLA Modules:
  0.0 70.5 jit_solution(4672756340840715677)
XLA Ops:
  0.0 1.4 %reshape.10.pot_ref = f32[8,128]{1,0:T(8,128)} reshape(f32[1,8,2,64]{3,2,1,0:T(2,128)} %param.3) | data formatting | bytes 8192 | tf_op jit(solution)/shard_map/reshape | solution.py:404
  1.4 66.9 %shard_map.28 = f32[16,128,128]{2,1,0:T(8,128)} custom-call(f32[16,128,128]{2,1,0:T(8,128)} %bitcast.5, f32[8,128]{1,0:T(8,128)} %reshape.10.pot_ref), custom_call_target="tpu_custom_call" | custom-call | tf_op jit(solution)/shard_map/pallas_call | solution.py:393
  68.2 2.3 %copy.5 = f32[2,1,8,2,64,128]{5,4,3,2,1,0:T(8,128)} copy(f32[2,1,8,2,64,128]{5,4,3,2,1,0:T(8,128)} %bitcast.4) | data formatting | bytes 2097152

commit v2 on v1

--- a/solution.py
+++ b/solution.py
@@ -122,8 +122,9 @@
 LANES = 128
 HALF = SUB // 2
 CHUNKS = 2
-UNROLL_A = 2
-UNROLL_B = 2
+GROUP = 4
+UNROLL_A = 4
+UNROLL_B = 8
 
 
 def swap_parts(x):
@@ -165,7 +166,7 @@
     return [zero if r is None else r for r in real], [zero if m is None else m for m in imag]
 
 
-def kernel(n, nx, nz, psi_ref, pot_ref, out_ref, send, recv, basis, outb, back, pots,
+def kernel(n, nx, nz, psi_ref, pot_ref, out_ref, send, recv, basis, outb, back, pots, mix,
            send_sem, recv_sem, pot_send, pot_recv, back_send, back_recv):
     me = lax.axis_index("dom")
     mesh_ids = pl.DeviceIdType.MESH
@@ -237,32 +238,39 @@
         pot_copy(there, there).wait_recv()
         return carry
 
-    lane = lax.broadcasted_iota(jnp.int32, (SUB, LANES), 1)
-    upper = lane >= nz
-    cell = lax.rem(lane, nz)
+    upper = lax.broadcasted_iota(jnp.int32, (SUB, LANES), 1) >= nz
     sign = jnp.where(lax.broadcasted_iota(jnp.int32, (SUB, LANES), 0) < HALF, 1.0, -1.0)
-    masks = {1: cell < 1, 2: cell < 2, -1: cell >= nz - 1, -2: cell >= nz - 2}
-    near, far = -0.5 * near_weight, -0.5 * far_weight
-    rotate = lambda u, by: pltpu.roll(u, by % LANES, 1)
-
-    def along_z(u, by):
-        return jnp.where(masks[by], rotate(u, by + nz), rotate(u, by))
+    ratio = -0.5 * far_weight
+
+    row = lax.broadcasted_iota(jnp.int32, (LANES, LANES), 0)
+    column = lax.broadcasted_iota(jnp.int32, (LANES, LANES), 1)
+    apart = lax.rem(row - column + 2 * nz, nz)
+    near_z = jnp.where(jnp.logical_or(apart == 1, apart == nz - 1), 16.0, 0.0)
+    far_z = jnp.where(jnp.logical_or(apart == 2, apart == nz - 2), 1.0, 0.0)
+    same = (row < nz) == (column < nz)
+    lanes_matrix = jnp.where(same, far_z - near_z, jnp.where(apart == 0, -16.0, 0.0)).astype(jnp.bfloat16)
+    mix[0:LANES] = lanes_matrix
+    mix[LANES:2 * LANES] = lanes_matrix
 
     def applied_at(ref, s):
-        before = [ref[s, x] for x in range(nx)]
-        now = [ref[s + 1, x] for x in range(nx)]
-        after = [ref[s + 2, x] for x in range(nx)]
+        slabs = [[ref[s + g, x] for x in range(nx)] for g in range(GROUP + 2)]
+        inner = jnp.concatenate([u for slab in slabs[1:-1] for u in slab], axis=0)
+        high = inner.astype(jnp.bfloat16)
+        rest = (inner - high.astype(jnp.float32)).astype(jnp.bfloat16)
+        mixed = jnp.dot(jnp.concatenate([high, rest], axis=1), mix[...], preferred_element_type=jnp.float32)
         result = []
-        for x in range(nx):
-            u = now[x]
-            close = now[(x + 1) % nx] + now[(x - 1) % nx]
-            close = close + rotate(u + jnp.where(upper, before[x], after[x]), nz)
-            close = close + along_z(u, 1) + along_z(u, -1)
-            wide = now[(x + 2) % nx] + now[(x - 2) % nx] + before[x] + after[x]
-            wide = wide + along_z(u, 2) + along_z(u, -2)
-            own = jnp.broadcast_to(pots[s, pl.ds(x, 1), :], (SUB, LANES)) + -0.5 * centre_weight
-            result.append(own * u + near * close + far * wide)
-        return now, result
+        for g in range(GROUP):
+            before, now, after = slabs[g:g + 3]
+            for x in range(nx):
+                u = now[x]
+                close = now[(x + 1) % nx] + now[(x - 1) % nx]
+                close = close + pltpu.roll(jnp.where(upper, before[x], after[x]), nz, 1)
+                wide = now[(x + 2) % nx] + now[(x - 2) % nx] + before[x] + after[x]
+                at = (g * nx + x) * SUB
+                wide = wide + mixed[at:at + SUB]
+                own = jnp.broadcast_to(pots[s + g, pl.ds(x, 1), :], (SUB, LANES)) + -0.5 * centre_weight
+                result.append((own * u + ratio * (wide - 16.0 * close), u))
+        return result
 
     def chunk(c, carry):
         vectors = [recv.at[c]] + [basis.at[j] for j in range(ITERS - 1)]
@@ -296,14 +304,13 @@
 
             def apply(s, accs, ref=ref, fresh=fresh):
                 accs = list(accs)
-                now, result = applied_at(ref, s)
-                for x in range(nx):
+                for at, (w, u) in enumerate(applied_at(ref, s * GROUP)):
                     if fresh is not None:
-                        fresh[s + 1, x] = result[x]
-                    accs[x % 2] = accs[x % 2] + now[x] * result[x]
+                        fresh[s * GROUP + at // nx + 1, at % nx] = w
+                    accs[at % 2] = accs[at % 2] + u * w
                 return tuple(accs)
 
-            accs = lax.fori_loop(0, n, apply, (zero, zero), unroll=UNROLL_A)
+            accs = lax.fori_loop(0, n // GROUP, apply, (zero, zero), unroll=UNROLL_A)
             scale = scales[j]
             alpha = scale * (scale * total_of(accs[0] + accs[1]))
             alphas.append(alpha)
@@ -397,7 +404,7 @@
         out_specs=pl.BlockSpec(memory_space=pltpu.VMEM),
         scratch_shapes=[
             vec(CHUNKS, n), vec(CHUNKS, n + 2), vec(ITERS - 1, n + 2), vec(CHUNKS, n), vec(CHUNKS, n),
-            pltpu.VMEM((n, nx, LANES), jnp.float32),
+            pltpu.VMEM((n, nx, LANES), jnp.float32), pltpu.VMEM((2 * LANES, LANES), jnp.bfloat16),
             dma(CHUNKS, n), dma(CHUNKS, n), dma(n), dma(n), dma(CHUNKS, n), dma(CHUNKS, n),
         ],
         compiler_params=pltpu.CompilerParams(collective_id=0, has_side_effects=True),
@@ -407,7 +414,7 @@
 
 def fits(psi, n):
     parts, slabs, nx, by, nz, orbs = psi.shape
-    return parts == 2 and slabs == 1 and by == 2 and by * nz == LANES and orbs == LANES and orbs == n * SUB and n > 1
+    return parts == 2 and slabs == 1 and by == 2 and by * nz == LANES and orbs == LANES and orbs == n * SUB and n % GROUP == 0
 
 
 def per_device(n, psi, potential):

time: 70.8 us -> 61.2 us (0.86)
  Pallas kernels: 66.9 us -> 57.2 us
    pallas_call x1, Pallas kernels: 66.9 us -> 57.2 us  [fused(): pl.pallas_call(functools.partial(kernel, n, nx, nz), out_shape=jax.ShapeD...]
where the time goes in v2:
time: 61.2 us; the launch traced here: 60.9 us
  Pallas kernels  57.2 us (93%)
  local copies, waits for them, and re-layouts  3.67 us (6%)
    pallas_call x1, Pallas kernels, fused(): pl.pallas_call(functools.partial(kernel, n, nx, nz), out_shape=jax.ShapeD...  57.2 us
    unnamed x1, local copies, waits for them, and re-layouts  2.31 us
    reshape x1, local copies, waits for them, and re-layouts, fused(): potential.reshape(nx, by * nz)  1.36 us

profile of v2, /device:TPU:28, one launch (start us, length us, event | category | flops | bytes accessed | tf_op | source)
XLA Modules:
  0.0 60.9 jit_solution(16181186897876224768)
XLA Ops:
  0.0 1.4 %reshape.10.pot_ref = f32[8,128]{1,0:T(8,128)} reshape(f32[1,8,2,64]{3,2,1,0:T(2,128)} %param.3) | data formatting | bytes 8192 | tf_op jit(solution)/shard_map/reshape | solution.py:411
  1.4 57.2 %shard_map.28 = f32[16,128,128]{2,1,0:T(8,128)} custom-call(f32[16,128,128]{2,1,0:T(8,128)} %bitcast.5, f32[8,128]{1,0:T(8,128)} %reshape.10.pot_ref), custom_call_target="tpu_custom_call" | custom-call | tf_op jit(solution)/shard_map/pallas_call | solution.py:400
  58.6 2.3 %copy.5 = f32[2,1,8,2,64,128]{5,4,3,2,1,0:T(8,128)} copy(f32[2,1,8,2,64,128]{5,4,3,2,1,0:T(8,128)} %bitcast.4) | data formatting | bytes 2097152
